TPU v7x, 256 devices: a whole 4x4x8 slice. The times are simulated.
256 devices in a mesh: client: 16 (over y_lo, z), tensor: 8 (over x, core), sdata: 2 (over y_hi).
Axes of the slice: x: 4, y: 4 (y_hi: 2, y_lo: 2; y = y_hi * 2 + y_lo), z: 8, core: 2. Of those that a mesh axis runs over, the one named last changes fastest.
Arguments:
- client_input: bfloat16 [12288, 2048], P(('client', 'sdata')), may hold values from -6 to 6
- client_gain: bfloat16 [16, 2048], P('client'), may hold values from 0.5 to 1.5
- query_weight: bfloat16 [16, 2048, 2048], P('client', None, 'tensor'), as said below
- key_weight: bfloat16 [16, 2048, 512], P('client', None, 'tensor'), as said below
- client_value_weight: bfloat16 [16, 2048, 512], P('client', None, 'tensor'), may hold values from -0.125 to 0.125
- output_weight: bfloat16 [16, 2048, 2048], P('client', None, 'tensor'), may hold values from -0.125 to 0.125
- server_gain: bfloat16 [2, 2048], P('sdata'), may hold values from 0.5 to 1.5
- server_gate: bfloat16 [2, 2048, 4096], P('sdata', None, 'tensor'), may hold values from -0.125 to 0.125
- server_up: bfloat16 [2, 2048, 4096], P('sdata', None, 'tensor'), may hold values from -0.125 to 0.125
- server_down: bfloat16 [2, 4096, 2048], P('sdata', 'tensor'), may hold values from -0.09375 to 0.09375
- upstream: bfloat16 [12288, 2048], P(('client', 'sdata')), may hold values from -6 to 6
- assignment: int32 [16], replicated, may hold values from 0 to 1, as said below
Outputs:
- query_update: bfloat16 [2048, 2048], P(('client', 'sdata'), 'tensor')
- key_update: bfloat16 [2048, 512], P(('client', 'sdata'), 'tensor')
- value_update: bfloat16 [2048, 512], P(('client', 'sdata'), 'tensor')
- output_update: bfloat16 [2048, 2048], P(('client', 'sdata'), 'tensor')
Inputs may be any that keep to these rules, and one draw needn't show every extreme that they name: `assignment`: each of the 2 server groups is named by exactly 8 clients. `query_weight`: independent entries with a spread of about 2048 ** -0.5. `key_weight`: entries with a spread of about 2048 ** -0.5 or more.
All inputs are finite; a program needn't handle non-finite values.
Results may differ from a plain program's by a relative error of at most 0.038.
The roundings to bfloat16 on the way count: a program that leaves them out, or rounds other values in their place, can miss the bound.
Values may be sent and summed in bfloat16 or wider, within the bound.
No kernel may reach another device: no remote copies, remote signals or barrier semaphores. Data moves between devices by JAX's collectives and lax.ppermute only.
A program may use at most 128 MiB of HBM per device.

v0:
```python
from functools import partial
import math
import jax
import jax.numpy as jnp
from jax import lax
from jax.sharding import PartitionSpec as P

HEAD_DIM = 64


def cut_along(value, dim, length):
    before, after = (value.shape[:dim], value.shape[dim + 1 :])
    return jnp.moveaxis(value.reshape(*before, length, -1, *after), dim, 0)


def sum_at_owner(value, axis, dim):
    length = lax.axis_size(axis)
    tiles = lax.all_to_all(cut_along(value, dim, length), axis, 0, 0, tiled=True)
    return jnp.sum(tiles.astype(jnp.float32), axis=0)


def rotary_tables(length):
    halfway = HEAD_DIM // 2
    positions = jnp.arange(length).astype(jnp.float32)
    exponents = jnp.arange(halfway).astype(jnp.float32) * (2.0 / HEAD_DIM)
    frequencies = jnp.exp(-math.log(500000.0) * exponents)
    angles = positions[:, None] * frequencies[None, :]
    cosine_table = jnp.concatenate([jnp.cos(angles), jnp.cos(angles)], 1)
    sine_table = jnp.concatenate([jnp.sin(angles), jnp.sin(angles)], 1)
    return (cosine_table, sine_table)


def rotary(heads_in, cosine_table, sine_table):
    halfway = heads_in.shape[-1] // 2
    turned = jnp.concatenate([-heads_in[..., halfway:], heads_in[..., :halfway]], -1)
    return heads_in * cosine_table[:, None, :] + turned * sine_table[:, None, :]


def normalize(rows_in, gain):
    rows_float = rows_in.astype(jnp.float32)
    inv_rms = lax.rsqrt(jnp.mean(rows_float * rows_float, -1, keepdims=True) + 1e-05)
    return (rows_float * inv_rms * gain.astype(jnp.float32)).astype(jnp.bfloat16)


def attention_part(normed, query_matrix, client_key_matrix, value_matrix, output_matrix):
    length = normed.shape[0]
    query_count = query_matrix.shape[1] // HEAD_DIM
    shared_count = client_key_matrix.shape[1] // HEAD_DIM
    group_size = query_count // shared_count
    cosine_table, sine_table = rotary_tables(length)
    queries = jnp.dot(normed, query_matrix, preferred_element_type=jnp.float32).reshape(
        length, query_count, HEAD_DIM
    )
    queries = (
        rotary(queries, cosine_table, sine_table)
        .astype(jnp.bfloat16)
        .reshape(length, shared_count, group_size, HEAD_DIM)
    )
    key_heads = jnp.dot(normed, client_key_matrix, preferred_element_type=jnp.float32).reshape(
        length, shared_count, HEAD_DIM
    )
    key_heads = rotary(key_heads, cosine_table, sine_table).astype(jnp.bfloat16)
    value_heads = (
        jnp.dot(normed, value_matrix, preferred_element_type=jnp.float32)
        .astype(jnp.bfloat16)
        .reshape(length, shared_count, HEAD_DIM)
    )
    scores = jnp.einsum(
        "qgrd,kgd->grqk", queries.astype(jnp.float32), key_heads.astype(jnp.float32)
    ) * HEAD_DIM ** (-0.5)
    row_ids = lax.broadcasted_iota(jnp.int32, (length, length), 0)
    col_ids = lax.broadcasted_iota(jnp.int32, (length, length), 1)
    scores = jnp.where(col_ids <= row_ids, scores, -1e30)
    highest = lax.stop_gradient(jnp.max(scores, -1, keepdims=True))
    exponent = jnp.exp(scores - highest)
    weights = (exponent / jnp.sum(exponent, -1, keepdims=True)).astype(jnp.bfloat16)
    context = jnp.einsum(
        "grqk,kgd->qgrd", weights.astype(jnp.float32), value_heads.astype(jnp.float32)
    )
    context = context.astype(jnp.bfloat16).reshape(length, query_count * HEAD_DIM)
    return lax.dot_general(
        context, output_matrix, (((1,), (1,)), ((), ())), preferred_element_type=jnp.float32
    )


def server_pull(rows_in, upstream_rows, gain, gate_matrix, up_matrix, down_matrix):
    rows_float = rows_in.astype(jnp.float32)
    inv_rms = lax.rsqrt(jnp.mean(rows_float * rows_float, -1, keepdims=True) + 1e-05)
    gain_float = gain.astype(jnp.float32)
    server_normed = (rows_float * inv_rms * gain_float).astype(jnp.bfloat16)
    gate_value = jnp.dot(server_normed, gate_matrix, preferred_element_type=jnp.float32)
    up_value = jnp.dot(server_normed, up_matrix, preferred_element_type=jnp.float32)
    pulled = lax.dot_general(
        upstream_rows, down_matrix, (((1,), (1,)), ((), ())), preferred_element_type=jnp.float32
    )
    sigmoid_gate = jax.nn.sigmoid(gate_value)
    gate_grad = (
        pulled * up_value * sigmoid_gate * (1.0 + gate_value * (1.0 - sigmoid_gate))
    ).astype(jnp.bfloat16)
    up_grad = (pulled * gate_value * sigmoid_gate).astype(jnp.bfloat16)
    normed_grad = lax.dot_general(
        gate_grad, gate_matrix, (((1,), (1,)), ((), ())), preferred_element_type=jnp.float32
    )
    normed_grad = normed_grad + lax.dot_general(
        up_grad, up_matrix, (((1,), (1,)), ((), ())), preferred_element_type=jnp.float32
    )
    weighted = normed_grad * gain_float
    return inv_rms * weighted - rows_float * inv_rms**3 * jnp.mean(
        weighted * rows_float, -1, keepdims=True
    )


def over_clients(pieces):
    return lax.all_to_all(pieces, "client", split_axis=1, concat_axis=1, tiled=True)


def over_groups(pieces):
    return lax.all_to_all(pieces, "sdata", split_axis=1, concat_axis=1, tiled=True)


def relay_out(stacked, group_order, client_count):
    count_rows, length, breadth = stacked.shape
    pieces = stacked.reshape(count_rows, client_count, length // client_count, breadth)
    arrived = jnp.take(over_clients(pieces), group_order, axis=1)
    return over_groups(arrived).reshape(count_rows, length, breadth)


def relay_back(stacked, inverse, client_count):
    count_rows, length, breadth = stacked.shape
    pieces = stacked.reshape(count_rows, client_count, length // client_count, breadth)
    arrived = jnp.take(over_groups(pieces), inverse, axis=1)
    return over_clients(arrived).reshape(count_rows, length, breadth)


def share_sum(partial_rows):
    return sum_at_owner(partial_rows.astype(jnp.bfloat16), "tensor", 1)


def widen_rows(stacked):
    return lax.all_gather(stacked, "tensor", axis=2, tiled=True)


def local(
    client_input,
    client_gain,
    query_weight,
    key_weight,
    client_value_weight,
    output_weight,
    server_gain,
    server_gate,
    server_up,
    server_down,
    upstream,
    assignment,
):
    client_count = lax.axis_size("client")
    normed = normalize(client_input, client_gain[0])
    attended, pullback = jax.vjp(
        partial(attention_part, normed),
        query_weight[0],
        key_weight[0],
        client_value_weight[0],
        output_weight[0],
    )
    group_order = jnp.argsort(assignment, stable=True)
    inverse = jnp.argsort(group_order, stable=True)
    shard_width = client_input.shape[1] // lax.axis_size("tensor")
    shard_start = lax.axis_index("tensor") * shard_width
    own_input = lax.dynamic_slice_in_dim(client_input, shard_start, shard_width, 1)
    own_upstream = lax.dynamic_slice_in_dim(upstream, shard_start, shard_width, 1)
    cut_input = (own_input.astype(jnp.float32) + share_sum(attended)).astype(jnp.bfloat16)
    arrived = relay_out(jnp.stack([cut_input, own_upstream]), group_order, client_count)
    widened = widen_rows(arrived)
    pulled = server_pull(
        widened[0], widened[1], server_gain[0], server_gate[0], server_up[0], server_down[0]
    )
    cut_grad = (share_sum(pulled) + arrived[1].astype(jnp.float32)).astype(jnp.bfloat16)
    returned = relay_back(cut_grad[None], inverse, client_count)
    arriving_grad = widen_rows(returned)[0]
    query_grad, key_grad, value_grad, output_grad = pullback(arriving_grad.astype(jnp.float32))
    query_width = query_grad.shape[1]
    key_width = key_grad.shape[1]
    joined_grads = jnp.concatenate(
        [
            query_grad.astype(jnp.float32),
            key_grad.astype(jnp.float32),
            value_grad.astype(jnp.float32),
            output_grad.astype(jnp.float32),
        ],
        1,
    )
    summed = sum_at_owner(joined_grads.astype(jnp.bfloat16), ("client", "sdata"), 0) / client_count
    query_update = summed[:, :query_width].astype(jnp.bfloat16)
    key_update = summed[:, query_width : query_width + key_width].astype(jnp.bfloat16)
    value_update = summed[:, query_width + key_width : query_width + 2 * key_width].astype(
        jnp.bfloat16
    )
    output_update = summed[:, query_width + 2 * key_width :].astype(jnp.bfloat16)
    return (query_update, key_update, value_update, output_update)


def solution(mesh):
    placed = (
        P(("client", "sdata"), None),
        P("client", None),
        P("client", None, "tensor"),
        P("client", None, "tensor"),
        P("client", None, "tensor"),
        P("client", None, "tensor"),
        P("sdata", None),
        P("sdata", None, "tensor"),
        P("sdata", None, "tensor"),
        P("sdata", "tensor", None),
        P(("client", "sdata"), None),
        P(),
    )
    return jax.shard_map(
        local,
        mesh=mesh,
        in_specs=placed,
        out_specs=(
            P(("client", "sdata"), "tensor"),
            P(("client", "sdata"), "tensor"),
            P(("client", "sdata"), "tensor"),
            P(("client", "sdata"), "tensor"),
        ),
        check_vma=False,
    )
```

profile of v0, /device:TPU:4, one launch (start us, length us, event | category | flops | bytes accessed | tf_op | source)
XLA Modules:
  0.0 317.1 jit_solution(7294213297382398546)
XLA Ops:
  7.3 0.8 mul.298
  8.1 1.9 fusion.3
  10.0 2.1 fusion.91
  12.2 1.4 copy.27
  13.6 2.6 fusion.36
  16.3 0.7 fusion.74
  17.9 0.7 copy-done.14
  18.6 0.6 fusion.31
  19.8 0.8 fusion.54
  20.7 0.6 copy-done.5
  21.3 0.6 convolution_convert_fusion
  21.9 1.2 copy.46
  23.1 6.4 %all-to-all-start = ((bf16[8,384,256]{2,1,0:T(8,128)(2,1)}), bf16[8,384,256]{2,1,0:T(8,128)(2,1)}, u32[]{:S(2)}, u32[]{:S(2)}) async-start(bf16[8,384,256]{2,1,0:T(8,128)(2,1)} %bitcast.249), calls=%async_computation | async-start | bytes 3145728 | tf_op jit(solution)/shard_map/all_to_all | solution.py:18
  29.6 1.0 constant_dynamic-slice_fusion
  30.5 17.5 %all-to-all-done = bf16[8,384,256]{2,1,0:T(8,128)(2,1)} async-done(((bf16[8,384,256]{2,1,0:T(8,128)(2,1)}), bf16[8,384,256]{2,1,0:T(8,128)(2,1)}, u32[]{:S(2)}, u32[]{:S(2)}) %all-to-all-start) | async-done | bytes 1572896 | tf_op jit(solution)/shard_map/all_to_all | solution.py:18
  48.1 1.7 convert_reduce_fusion.2
  49.7 1.0 add_convert_fusion.1
  50.7 0.8 pad_maximum_fusion.1
  51.5 8.0 %all-to-all-start.1 = ((bf16[2,16,24,256]{3,2,0,1:T(8,128)(2,1)}), bf16[2,16,24,256]{3,2,0,1:T(8,128)(2,1)S(1)}, u32[]{:S(2)}, u32[]{:S(2)}) async-start(bf16[2,16,24,256]{3,2,0,1:T(8,128)(2,1)} %pad_maximum_fusion.1), calls=%async_computation.1 | async-start | bytes 786432 | tf_op jit(solution)/shard_map/all_to_all | solution.py:114
  59.6 1.3 sort.31
  60.9 0.6 compare_select_fusion
  61.5 0.6 compare_and_fusion
  62.1 10.1 %all-to-all-done.1 = bf16[2,16,24,256]{3,2,0,1:T(8,128)(2,1)S(1)} async-done(((bf16[2,16,24,256]{3,2,0,1:T(8,128)(2,1)}), bf16[2,16,24,256]{3,2,0,1:T(8,128)(2,1)S(1)}, u32[]{:S(2)}, u32[]{:S(2)}) %all-to-all-start.1) | async-done | bytes 393248 | tf_op jit(solution)/shard_map/all_to_all | solution.py:114
  72.2 0.8 copy.30
  73.0 1.6 gather_fusion
  74.6 11.3 %all_to_all.35 = bf16[2,16,24,256]{3,2,0,1:T(8,128)(2,1)S(1)} all-to-all(bf16[2,16,24,256]{3,2,0,1:T(8,128)(2,1)S(1)} %select_bitcast_fusion), channel_id=1, replica_groups=mesh['client'=16,'tensor'=8,'sdata'=2] {'sdata'}, dimensions={1} | all-to-all | bytes 786432 | tf_op jit(solution)/shard_map/all_to_all | solution.py:118
  86.0 0.8 copy.31
  86.8 0.7 mul.299
  87.5 29.4 %all-gather.3.cloned.1.call-done = bf16[2,384,2048]{2,1,0:T(8,128)(2,1)} async-done(((bf16[2,384,256]{2,1,0:T(8,128)(2,1)}), bf16[2,384,2048]{2,1,0:T(8,128)(2,1)}) %all-gather.3.cloned.1.call-update) | async-done | bytes 3145744 | tf_op jit(solution)/shard_map/all_gather | solution.py:140
  116.9 1.8 fusion.6
  118.7 0.6 multiply_multiply_fusion
  119.3 4.1 %fusion.29 = f32[384,512]{1,0:T(8,128)} fusion(bf16[1,512,2048]{2,1,0:T(8,128)(2,1)} %param.21, bf16[2,384,2048]{2,1,0:T(8,128)(2,1)} %all-gather.3.cloned.1.call-done), kind=kOutput, calls=%fused_computation.50 | convolution fusion | flops 805306368 | bytes 4456448 | tf_op jit(solution)/shard_map/dot_general | solution.py:93
  123.5 1.9 fusion.24
  125.4 6.3 %fusion.22 = f32[384,2048]{1,0:T(8,128)} fusion(bf16[1,2048,512]{2,1,0:T(8,128)(2,1)} %param.19, f32[384,512]{1,0:T(8,128)} %fusion.29, bf16[1,2048,512]{2,1,0:T(8,128)(2,1)S(1)} %copy-done, f32[384,512]{1,0:T(8,128)} %fusion.24, f32[2048]{0:T(1024)S(1)} %bitcast.271, f32[384]{0:T(512)} %copy-done.29, bf16[2,384,2048]{2,1,0:T(8,128)(2,1)} %all-gather.3.cloned.1.call-done), kind=kOutput, calls=%fused_computation.43 | convolution fusion | flops 1615724544 | bytes 10496000 | tf_op jit(solution)/shard_map/dot_general | solution.py:101
  131.7 4.2 %fusion.10 = (f32[384]{0:T(512)S(1)}, f32[384,2048]{1,0:T(8,128)S(1)}) fusion(bf16[2,384,2048]{2,1,0:T(8,128)(2,1)} %all-gather.3.cloned.1.call-done, f32[2048]{0:T(1024)S(1)} %bitcast.272, f32[384,2048]{1,0:T(8,128)} %fusion.22, bf16[1,2048,512]{2,1,0:T(8,128)(2,1)S(1)} %copy-done, f32[384,512]{1,0:T(8,128)} %fusion.29, f32[384,512]{1,0:T(8,128)} %fusion.24), kind=kOutput, calls=%fused_computation.17 | convolution fusion | flops 810417792 | bytes 11544064 | tf_op jit(solution)/shard_map/dot_general | solution.py:104
  135.9 0.6 fusion.9
  136.5 1.2 copy.45
  137.8 5.0 %all-to-all-start.3 = ((bf16[8,384,256]{2,1,0:T(8,128)(2,1)}), bf16[8,384,256]{2,1,0:T(8,128)(2,1)}, u32[]{:S(2)}, u32[]{:S(2)}) async-start(bf16[8,384,256]{2,1,0:T(8,128)(2,1)} %bitcast.250), calls=%async_computation.3 | async-start | bytes 3145728 | tf_op jit(solution)/shard_map/all_to_all | solution.py:18
  143.3 1.9 sort.32
  145.2 1.2 compare_select_fusion.1
  146.4 1.2 compare_and_fusion.1
  147.5 13.8 %all-to-all-done.3 = bf16[8,384,256]{2,1,0:T(8,128)(2,1)} async-done(((bf16[8,384,256]{2,1,0:T(8,128)(2,1)}), bf16[8,384,256]{2,1,0:T(8,128)(2,1)}, u32[]{:S(2)}, u32[]{:S(2)}) %all-to-all-start.3) | async-done | bytes 1572896 | tf_op jit(solution)/shard_map/all_to_all | solution.py:18
  161.3 1.7 convert_reduce_fusion.1
  163.0 0.7 add_convert_fusion
  163.7 4.4 %all-to-all-start.4 = ((bf16[1,16,24,256]{3,2,0,1:T(8,128)(2,1)}), bf16[1,16,24,256]{3,2,0,1:T(8,128)(2,1)S(1)}, u32[]{:S(2)}, u32[]{:S(2)}) async-start(bf16[1,16,24,256]{3,2,0,1:T(8,128)(2,1)} %add_convert_fusion), calls=%async_computation.4 | async-start | bytes 393216 | tf_op jit(solution)/shard_map/all_to_all | solution.py:118
  168.1 0.7 pad_clamp_fusion
  168.8 5.7 %all-to-all-done.4 = bf16[1,16,24,256]{3,2,0,1:T(8,128)(2,1)S(1)} async-done(((bf16[1,16,24,256]{3,2,0,1:T(8,128)(2,1)}), bf16[1,16,24,256]{3,2,0,1:T(8,128)(2,1)S(1)}, u32[]{:S(2)}, u32[]{:S(2)}) %all-to-all-start.4) | async-done | bytes 196640 | tf_op jit(solution)/shard_map/all_to_all | solution.py:118
  174.4 1.2 gather_fusion.1
  175.7 1.0 fusion.94
  176.7 15.7 %all_to_all.36 = bf16[1,16,24,256]{3,2,0,1:T(8,128)(2,1)} all-to-all(bf16[1,16,24,256]{3,2,0,1:T(8,128)(2,1)S(1)} %fusion.94), channel_id=1, replica_groups=mesh['client'=16,'tensor'=8,'sdata'=2] {'client'}, dimensions={1} | all-to-all | bytes 393216 | tf_op jit(solution)/shard_map/all_to_all | solution.py:114
  192.5 23.7 %all-gather.5.cloned.1.call-done = bf16[1,384,2048]{2,1,0:T(8,128)(2,1)} async-done(((bf16[1,384,256]{2,1,0:T(8,128)(2,1)}), bf16[1,384,2048]{2,1,0:T(8,128)(2,1)}) %all-gather.5.cloned.1.call-update) | async-done | bytes 1572880 | tf_op jit(solution)/shard_map/all_gather | solution.py:140
  216.2 2.3 fusion.57
  218.5 1.7 fusion.21
  220.3 1.1 broadcast_multiply_fusion
  221.4 1.2 fusion.68
  222.7 4.1 %convolution_convert_fusion.3 = bf16[2048,64]{0,1:T(8,128)(2,1)} fusion(bf16[64,4,384]{2,0,1:T(8,128)(2,1)S(1)} %bitcast.269, f32[4,384]{1,0:T(4,128)S(1)} %copy-done.27, f32[4,384]{1,0:T(4,128)S(1)} %get-tuple-element.27, f32[384,384,4]{1,0,2:T(8,128)} %copy-done.1, pred[384,384]{0,1:T(8,128)(4,1)S(1)} %copy-done.9, bf16[384,2048]{1,0:T(8,128)(2,1)} %param.12, ...), kind=kOutput, calls=%fused_computation.41 | convolution fusion | flops 182411264 | bytes 4560384 | tf_op jit(solution)/shard_map/transpose(jvp())/dot_general | solution.py:64
  226.9 3.4 %convolution_convert_fusion.2 = bf16[2048,256]{1,0:T(8,128)(2,1)} fusion(bf16[384,256]{0,1:T(8,128)(2,1)S(1)} %bitcast.267, bf16[384,2048]{1,0:T(8,128)(2,1)} %param.12, f32[2048]{0:T(1024)S(1)} %bitcast.277, f32[384]{0:T(512)S(1)} %copy-done.34), kind=kOutput, calls=%fused_computation.28 | convolution fusion | flops 405798912 | bytes 2827776 | tf_op jit(solution)/shard_map/transpose(jvp())/dot_general | solution.py:51
  230.4 0.6 convolution_convert_fusion.4
  231.3 1.2 copy.40
  232.5 2.2 convolution_convert_fusion.1
  234.8 1.3 pad_maximum_fusion
  236.0 72.6 %all_to_all.37 = bf16[32,64,640]{2,1,0:T(8,128)(2,1)S(1)} all-to-all(bf16[32,64,640]{2,1,0:T(8,128)(2,1)S(1)} %pad_maximum_fusion), channel_id=1, replica_groups=mesh['client'=16,'tensor'=8,'sdata'=2] {'client','sdata'}, dimensions={0} | all-to-all | bytes 5242880 | tf_op jit(solution)/shard_map/all_to_all | solution.py:18
  309.0 0.6 fusion.122
  309.6 0.7 fusion.123
  (104 shorter events, 3.2 us)
Async XLA Ops:
  7.2 118.2 %copy-start = (bf16[1,2048,512]{2,1,0:T(8,128)(2,1)S(1)}, bf16[1,2048,512]{2,1,0:T(8,128)(2,1)}, u32[]{:S(2)}) copy-start(bf16[1,2048,512]{2,1,0:T(8,128)(2,1)} %param.20) | copy-start | bytes 6291460
  7.3 12.5 %copy-start.8 = (pred[384,384]{0,1:T(8,128)(4,1)}, pred[384,384]{0,1:T(8,128)(4,1)S(1)}, u32[]{:S(2)}) copy-start(pred[384,384]{0,1:T(8,128)(4,1)S(1)} %iota_compare_fusion) | copy-start | bytes 442372
  8.1 8.2 %copy-start.31 = (f32[1,2048]{1,0:T(1,128)}, f32[1,2048]{1,0:T(1,128)S(1)}, u32[]{:S(2)}) copy-start(f32[1,2048]{1,0:T(1,128)S(1)} %mul.298) | copy-start | bytes 24580
  8.1 4.0 %copy-start.10 = (bf16[1,2048,256]{2,1,0:T(8,128)(2,1)S(1)}, bf16[1,2048,256]{2,1,0:T(8,128)(2,1)}, u32[]{:S(2)}) copy-start(bf16[1,2048,256]{2,1,0:T(8,128)(2,1)} %param.14) | copy-start | bytes 3145732
  10.0 6.2 %copy-start.33 = (f32[384]{0:T(512)}, f32[384]{0:T(512)S(1)}, u32[]{:S(2)}) copy-start(f32[384]{0:T(512)S(1)} %add_rsqrt_fusion.1) | copy-start | bytes 4612
  13.6 2.7 copy-start.6
  13.6 2.7 copy-start.36
  17.0 2.8 copy-start.38
  17.2 2.0 copy-start.18
  17.3 2.0 copy-start.22
  17.3 0.7 copy-start.12
  17.3 1.9 copy-start.20
  17.3 1.9 copy-start.24
  17.9 0.7 copy-start.14
  19.2 1.5 copy-start.1
  19.8 0.9 copy-start.26
  19.8 1.5 copy-start.5
  20.7 2.4 copy-start.16
  23.1 24.9 %all-to-all-start = ((bf16[8,384,256]{2,1,0:T(8,128)(2,1)}), bf16[8,384,256]{2,1,0:T(8,128)(2,1)}, u32[]{:S(2)}, u32[]{:S(2)}) async-start(bf16[8,384,256]{2,1,0:T(8,128)(2,1)} %bitcast.249), calls=%async_computation | async-start | bytes 3145728 | tf_op jit(solution)/shard_map/all_to_all | solution.py:18
  29.5 30.0 %copy-start.37 = (s32[16]{0:T(128)S(1)}, s32[16]{0:T(128)}, u32[]{:S(2)}) copy-start(s32[16]{0:T(128)} %param.23) | copy-start | bytes 196
  51.5 20.7 %all-to-all-start.1 = ((bf16[2,16,24,256]{3,2,0,1:T(8,128)(2,1)}), bf16[2,16,24,256]{3,2,0,1:T(8,128)(2,1)S(1)}, u32[]{:S(2)}, u32[]{:S(2)}) async-start(bf16[2,16,24,256]{3,2,0,1:T(8,128)(2,1)} %pad_maximum_fusion.1), calls=%async_computation.1 | async-start | bytes 786432 | tf_op jit(solution)/shard_map/all_to_all | solution.py:114
  59.5 57.4 %all-gather.3.cloned.1.call-start = ((), (), s32[]{:S(2)}) async-start(), calls=%async_computation.7 | async-start | bytes 3538944 | tf_op jit(solution)/shard_map/all_gather | solution.py:140
  119.3 4.2 %copy-start.29 = (f32[384]{0:T(512)}, f32[384]{0:T(512)S(1)}, u32[]{:S(2)}) copy-start(f32[384]{0:T(512)S(1)} %get-tuple-element.26) | copy-start | bytes 4612
  119.3 4.2 %copy-start.3 = (bf16[2,384,2048]{2,1,0:T(8,128)(2,1)S(1)}, bf16[2,384,2048]{2,1,0:T(8,128)(2,1)}, u32[]{:S(2)}) copy-start(bf16[2,384,2048]{2,1,0:T(8,128)(2,1)} %all-gather.3.cloned.1.call-done) | copy-start | bytes 9437188
  119.3 4.2 %copy-start.35 = (bf16[1,2048,512]{2,1,0:T(8,128)(2,1)S(1)}, bf16[1,2048,512]{2,1,0:T(8,128)(2,1)}, u32[]{:S(2)}) copy-start(bf16[1,2048,512]{2,1,0:T(8,128)(2,1)} %param.19) | copy-start | bytes 6291460
  131.6 4.2 %copy-start.4 = (bf16[2,384,2048]{2,1,0:T(8,128)(2,1)S(1)}, bf16[2,384,2048]{2,1,0:T(8,128)(2,1)}, u32[]{:S(2)}) copy-start(bf16[2,384,2048]{2,1,0:T(8,128)(2,1)} %all-gather.3.cloned.1.call-done) | copy-start | bytes 9437188
  131.6 4.2 %copy-start.28 = (f32[384]{0:T(512)S(1)}, f32[384]{0:T(512)}, u32[]{:S(2)}) copy-start(f32[384]{0:T(512)} %get-tuple-element.25) | copy-start | bytes 4612
  131.7 4.2 %copy-start.30 = (f32[384]{0:T(512)S(1)}, f32[384]{0:T(512)}, u32[]{:S(2)}) copy-start(f32[384]{0:T(512)} %copy-done.29) | copy-start | bytes 4612
  137.8 23.5 %all-to-all-start.3 = ((bf16[8,384,256]{2,1,0:T(8,128)(2,1)}), bf16[8,384,256]{2,1,0:T(8,128)(2,1)}, u32[]{:S(2)}, u32[]{:S(2)}) async-start(bf16[8,384,256]{2,1,0:T(8,128)(2,1)} %bitcast.250), calls=%async_computation.3 | async-start | bytes 3145728 | tf_op jit(solution)/shard_map/all_to_all | solution.py:18
  142.8 49.7 %copy-start.27 = (f32[4,384]{1,0:T(4,128)S(1)}, f32[4,384]{1,0:T(4,128)}, u32[]{:S(2)}) copy-start(f32[4,384]{1,0:T(4,128)} %copy-done.26) | copy-start | bytes 18436
  163.7 54.8 %copy-start.9 = (pred[384,384]{0,1:T(8,128)(4,1)S(1)}, pred[384,384]{0,1:T(8,128)(4,1)}, u32[]{:S(2)}) copy-start(pred[384,384]{0,1:T(8,128)(4,1)} %copy-done.8) | copy-start | bytes 442372
  163.7 10.7 %all-to-all-start.4 = ((bf16[1,16,24,256]{3,2,0,1:T(8,128)(2,1)}), bf16[1,16,24,256]{3,2,0,1:T(8,128)(2,1)S(1)}, u32[]{:S(2)}, u32[]{:S(2)}) async-start(bf16[1,16,24,256]{3,2,0,1:T(8,128)(2,1)} %add_convert_fusion), calls=%async_computation.4 | async-start | bytes 393216 | tf_op jit(solution)/shard_map/all_to_all | solution.py:118
  168.1 48.0 %all-gather.5.cloned.1.call-start = ((), (), s32[]{:S(2)}) async-start(), calls=%async_computation.8 | async-start | bytes 1769472 | tf_op jit(solution)/shard_map/all_gather | solution.py:140
  216.2 2.3 copy-start.2
  218.5 1.8 copy-start.21
  218.5 1.8 copy-start.25
  220.3 1.1 copy-start.15
  221.4 1.2 copy-start.32
  221.4 1.2 copy-start.34
  222.7 4.2 %copy-start.13 = (f32[384,64]{0,1:T(8,128)S(1)}, f32[384,64]{0,1:T(8,128)}, u32[]{:S(2)}) copy-start(f32[384,64]{0,1:T(8,128)} %copy-done.12) | copy-start | bytes 294916
  226.8 3.5 %copy-start.19 = (f32[384,32]{0,1:T(8,128)S(1)}, f32[384,32]{0,1:T(8,128)}, u32[]{:S(2)}) copy-start(f32[384,32]{0,1:T(8,128)} %copy-done.18) | copy-start | bytes 147460
  226.9 3.5 %copy-start.7 = (bf16[384,2048]{1,0:T(8,128)(2,1)S(1)}, bf16[384,2048]{1,0:T(8,128)(2,1)}, u32[]{:S(2)}) copy-start(bf16[384,2048]{1,0:T(8,128)(2,1)} %param.12) | copy-start | bytes 4718596
  226.9 3.5 %copy-start.23 = (f32[384,32]{0,1:T(8,128)S(1)}, f32[384,32]{0,1:T(8,128)}, u32[]{:S(2)}) copy-start(f32[384,32]{0,1:T(8,128)} %copy-done.22) | copy-start | bytes 147460
  230.3 2.2 copy-start.17
  232.5 2.3 copy-start.11
Sparse Core Ops, SparseCore 0:
  86.9 29.9 all-gather.2
  192.6 23.5 all-gather.4
where the time goes:
time: 318 us; the launch traced here: 317 us
  waiting for transfers between devices  100 us (31%)
  blocking collectives  99.6 us (31%)
  matrix products  40.7 us (13%)
  starting transfers between devices  23.9 us (8%)
  other arithmetic  23.6 us (7%)
  between operations  14.7 us (5%)
  local copies, waits for them, and re-layouts  14.5 us (5%)
    all_to_all x1, blocking collectives, sum_at_owner(): lax.all_to_all(cut_along(value, dim, length), axis, 0, 0, tiled=True)  72.6 us
    all_gather x2, waiting for transfers between devices, widen_rows(): return lax.all_gather(stacked, 'tensor', axis=2, tiled=True)  53.1 us
    all_to_all x2, waiting for transfers between devices, sum_at_owner(): lax.all_to_all(cut_along(value, dim, length), axis, 0, 0, tiled=True)  31.3 us
    all_to_all x1, blocking collectives, over_clients(): lax.all_to_all(pieces, 'client', split_axis=1, concat_axis=1, tiled=True)  15.7 us
    all_to_all x2, starting transfers between devices, sum_at_owner(): lax.all_to_all(cut_along(value, dim, length), axis, 0, 0, tiled=True)  11.4 us
    all_to_all x1, blocking collectives, over_groups(): lax.all_to_all(pieces, 'sdata', split_axis=1, concat_axis=1, tiled=True)  11.3 us
    all_to_all x1, waiting for transfers between devices, over_clients(): lax.all_to_all(pieces, 'client', split_axis=1, concat_axis=1, tiled=True)  10.1 us
    all_to_all x1, starting transfers between devices, over_clients(): lax.all_to_all(pieces, 'client', split_axis=1, concat_axis=1, tiled=True)  8.01 us
  transfers between devices with their start and end apart: 6, of which 6 were waited for; matrix products, arithmetic and copies ran while one was open for 3% of the time, Pallas kernels for 0%

commit v1 on v0

--- a/solution.py
+++ b/solution.py
@@ -137,7 +137,9 @@
 
 
 def widen_rows(stacked):
-    return lax.all_gather(stacked, "tensor", axis=2, tiled=True)
+    return jnp.concatenate(
+        lax.all_to_all(jnp.stack([stacked] * lax.axis_size("tensor")), "tensor", 0, 0), axis=2
+    )
 
 
 def local(

time: 318 us -> 330 us (1.038)
  starting transfers between devices: 23.9 us -> 38.7 us
  between operations: 14.7 us -> 1.26 us
  local copies, waits for them, and re-layouts: 14.5 us -> 24.6 us
  blocking collectives: 99.6 us -> 90.5 us
  waiting for transfers between devices: 100 us -> 106 us
    all_to_all x0 -> x2, waiting for transfers between devices: none -> 53.7 us  [widen_rows(): lax.all_to_all(jnp.stack([stacked] * lax.axis_size('tensor')), 'tensor',...]
    all_gather x2 -> x0, waiting for transfers between devices: 53.1 us -> none  [widen_rows(): return lax.all_gather(stacked, 'tensor', axis=2, tiled=True)]
    all_to_all x0 -> x2, starting transfers between devices: none -> 14.2 us  [widen_rows(): lax.all_to_all(jnp.stack([stacked] * lax.axis_size('tensor')), 'tensor',...]
    all_to_all x1, blocking collectives: 72.6 us -> 66.2 us  [sum_at_owner(): lax.all_to_all(cut_along(value, dim, length), axis, 0, 0, tiled=True)]
    all_to_all x0 -> x1, local copies, waits for them, and re-layouts: none -> 4.67 us  [widen_rows(): lax.all_to_all(jnp.stack([stacked] * lax.axis_size('tensor')), 'tensor',...]
    slice x0 -> x1, other arithmetic: none -> 4.46 us  [local(): widened[1]]
    convert_element_type x0 -> x1, local copies, waits for them, and re-layouts: none -> 3.58 us  [server_pull(): rows_float = rows_in.astype(jnp.float32)]
    another operation x0 -> x3, local copies, waits for them, and re-layouts: none -> 3.47 us  [widen_rows(): jnp.stack([stacked] * lax.axis_size('tensor'))]
  transfers between devices with their start and end apart: 6 -> 6, of which waited for: 6 -> 6; matrix products, arithmetic and copies ran while one was open for 3% -> 1% of each run, Pallas kernels for 0% -> 0%
where the time goes in v1:
time: 330 us; the launch traced here: 326 us
  waiting for transfers between devices  106 us (32%)
  blocking collectives  90.5 us (27%)
  matrix products  39.5 us (12%)
  starting transfers between devices  38.7 us (12%)
  other arithmetic  25.8 us (8%)
  local copies, waits for them, and re-layouts  24.6 us (7%)
    all_to_all x1, blocking collectives, sum_at_owner(): lax.all_to_all(cut_along(value, dim, length), axis, 0, 0, tiled=True)  66.2 us
    all_to_all x2, waiting for transfers between devices, widen_rows(): lax.all_to_all(jnp.stack([stacked] * lax.axis_size('tensor')), 'tensor',...  53.7 us
    all_to_all x2, waiting for transfers between devices, sum_at_owner(): lax.all_to_all(cut_along(value, dim, length), axis, 0, 0, tiled=True)  34.7 us
    all_to_all x2, starting transfers between devices, widen_rows(): lax.all_to_all(jnp.stack([stacked] * lax.axis_size('tensor')), 'tensor',...  14.2 us
    all_to_all x2, starting transfers between devices, sum_at_owner(): lax.all_to_all(cut_along(value, dim, length), axis, 0, 0, tiled=True)  13.1 us
    all_to_all x1, blocking collectives, over_clients(): lax.all_to_all(pieces, 'client', split_axis=1, concat_axis=1, tiled=True)  12.9 us
    all_to_all x1, waiting for transfers between devices, over_clients(): lax.all_to_all(pieces, 'client', split_axis=1, concat_axis=1, tiled=True)  11.4 us
    all_to_all x1, blocking collectives, over_groups(): lax.all_to_all(pieces, 'sdata', split_axis=1, concat_axis=1, tiled=True)  11.3 us
  transfers between devices with their start and end apart: 6, of which 6 were waited for; matrix products, arithmetic and copies ran while one was open for 1% of the time, Pallas kernels for 0%

profile of v1, /device:TPU:4, one launch (start us, length us, event | category | flops | bytes accessed | tf_op | source)
XLA Modules:
  0.0 326.4 jit_solution(9785524748324022834)
XLA Ops:
  0.7 1.9 fusion
  2.7 0.7 mul.299
  3.4 2.7 fusion.57
  6.2 0.7 fusion.71
  6.8 0.6 copy-done.16
  7.5 0.6 fusion.84
  8.1 1.4 copy.47
  9.6 2.5 fusion.22
  12.6 0.7 copy-done.12
  14.4 0.8 fusion.40
  15.2 0.6 copy-done.10
  15.9 0.6 convolution_convert_fusion
  16.5 1.2 copy.71
  17.8 6.4 %all-to-all-start = ((bf16[8,384,256]{2,1,0:T(8,128)(2,1)}), bf16[8,384,256]{2,1,0:T(8,128)(2,1)}, u32[]{:S(2)}, u32[]{:S(2)}) async-start(bf16[8,384,256]{2,1,0:T(8,128)(2,1)} %bitcast.234), calls=%async_computation | async-start | bytes 3145728 | tf_op jit(solution)/shard_map/all_to_all | solution.py:18
  24.2 1.0 constant_dynamic-slice_fusion
  25.1 17.5 %all-to-all-done = bf16[8,384,256]{2,1,0:T(8,128)(2,1)} async-done(((bf16[8,384,256]{2,1,0:T(8,128)(2,1)}), bf16[8,384,256]{2,1,0:T(8,128)(2,1)}, u32[]{:S(2)}, u32[]{:S(2)}) %all-to-all-start) | async-done | bytes 1572896 | tf_op jit(solution)/shard_map/all_to_all | solution.py:18
  42.7 1.7 convert_reduce_fusion.2
  44.3 1.0 add_convert_fusion.1
  45.3 0.8 pad_maximum_fusion.1
  46.1 8.0 %all-to-all-start.1 = ((bf16[2,16,24,256]{3,2,0,1:T(8,128)(2,1)}), bf16[2,16,24,256]{3,2,0,1:T(8,128)(2,1)S(1)}, u32[]{:S(2)}, u32[]{:S(2)}) async-start(bf16[2,16,24,256]{3,2,0,1:T(8,128)(2,1)} %pad_maximum_fusion.1), calls=%async_computation.1 | async-start | bytes 786432 | tf_op jit(solution)/shard_map/all_to_all | solution.py:114
  54.1 1.2 sort.31
  55.4 11.4 %all-to-all-done.1 = bf16[2,16,24,256]{3,2,0,1:T(8,128)(2,1)S(1)} async-done(((bf16[2,16,24,256]{3,2,0,1:T(8,128)(2,1)}), bf16[2,16,24,256]{3,2,0,1:T(8,128)(2,1)S(1)}, u32[]{:S(2)}, u32[]{:S(2)}) %all-to-all-start.1) | async-done | bytes 393248 | tf_op jit(solution)/shard_map/all_to_all | solution.py:114
  67.5 11.3 %all_to_all.45 = bf16[2,16,24,256]{3,2,0,1:T(8,128)(2,1)S(1)} all-to-all(bf16[2,16,24,256]{3,2,0,1:T(8,128)(2,1)S(1)} %select_bitcast_fusion), channel_id=1, replica_groups=mesh['client'=16,'tensor'=8,'sdata'=2] {'sdata'}, dimensions={1} | all-to-all | bytes 786432 | tf_op jit(solution)/shard_map/all_to_all | solution.py:118
  78.9 2.0 stack.18
  80.9 7.3 %all-to-all-start.3 = ((bf16[8,2,384,256]{3,2,1,0:T(8,128)(2,1)}), bf16[8,2,384,256]{3,2,1,0:T(8,128)(2,1)}, u32[]{:S(2)}, u32[]{:S(2)}) async-start(bf16[8,2,384,256]{3,2,1,0:T(8,128)(2,1)} %stack.18), calls=%async_computation.3 | async-start | bytes 6291456 | tf_op jit(solution)/shard_map/all_to_all | solution.py:141
  88.2 35.3 %all-to-all-done.3 = bf16[8,2,384,256]{3,2,1,0:T(8,128)(2,1)} async-done(((bf16[8,2,384,256]{3,2,1,0:T(8,128)(2,1)}), bf16[8,2,384,256]{3,2,1,0:T(8,128)(2,1)}, u32[]{:S(2)}, u32[]{:S(2)}) %all-to-all-start.3) | async-done | bytes 3145760 | tf_op jit(solution)/shard_map/all_to_all | solution.py:141
  123.5 4.7 %copy.52 = bf16[8,2,384,256]{2,3,0,1:T(8,128)(2,1)} copy(bf16[8,2,384,256]{3,2,1,0:T(8,128)(2,1)} %all-to-all-done.3) | data formatting | bytes 6291456 | tf_op jit(solution)/shard_map/all_to_all | solution.py:141
  128.2 1.8 multiply_reduce_fusion.1
  130.0 4.5 %fusion.100 = (bf16[1,384,8,256]{1,3,2,0:T(8,128)(2,1)}, f32[1,384,8,256]{1,3,2,0:T(8,128)}) fusion(bf16[2,384,8,256]{1,3,2,0:T(8,128)(2,1)} %bitcast.231), kind=kLoop, calls=%fused_computation.141 | loop fusion | flops 786432 | bytes 7864320 | tf_op jit(solution)/shard_map/slice | solution.py:178
  134.5 3.6 %copy.63 = f32[384,2048]{1,0:T(8,128)} copy(f32[384,2048]{0,1:T(8,128)} %bitcast.233) | data formatting | bytes 6291456 | tf_op jit(solution)/shard_map/convert_element_type | solution.py:87
  138.0 2.0 multiply_convert_fusion
  140.1 2.0 fusion.14
  142.1 0.9 copy-done.30
  143.0 2.0 fusion.19
  145.0 6.3 %fusion.12 = f32[384,2048]{1,0:T(8,128)} fusion(bf16[1,2048,512]{2,1,0:T(8,128)(2,1)} %param.19, f32[384,512]{1,0:T(8,128)} %fusion.19, bf16[384,2048]{0,1:T(8,128)(2,1)} %bitcast.244, bf16[1,2048,512]{2,1,0:T(8,128)(2,1)S(1)} %copy-done, f32[384,512]{1,0:T(8,128)} %fusion.14), kind=kOutput, calls=%fused_computation.35 | convolution fusion | flops 1612578816 | bytes 10485760 | tf_op jit(solution)/shard_map/dot_general | solution.py:101
  151.2 4.6 %multiply_reduce_fusion = (f32[384]{0:T(512)S(1)}, f32[384,2048]{1,0:T(8,128)S(1)}) fusion(f32[384,2048]{1,0:T(8,128)} %copy.63, f32[2048]{0:T(1024)S(1)} %bitcast.257, f32[384,2048]{1,0:T(8,128)} %fusion.12, bf16[1,2048,512]{2,1,0:T(8,128)(2,1)S(1)} %copy-done, f32[384,512]{1,0:T(8,128)} %fusion.19, f32[384,512]{1,0:T(8,128)} %fusion.14), kind=kOutput, calls=%fused_computation.10 | convolution fusion | flops 809631360 | bytes 13116928 | tf_op jit(solution)/shard_map/dot_general | solution.py:104
  156.4 1.3 copy.70
  157.7 6.7 %all-to-all-start.4 = ((bf16[8,384,256]{2,1,0:T(8,128)(2,1)}), bf16[8,384,256]{2,1,0:T(8,128)(2,1)S(1)}, u32[]{:S(2)}, u32[]{:S(2)}) async-start(bf16[8,384,256]{2,1,0:T(8,128)(2,1)} %bitcast.227), calls=%async_computation.4 | async-start | bytes 3145728 | tf_op jit(solution)/shard_map/all_to_all | solution.py:18
  164.4 1.2 sort.32
  165.7 17.1 %all-to-all-done.4 = bf16[8,384,256]{2,1,0:T(8,128)(2,1)S(1)} async-done(((bf16[8,384,256]{2,1,0:T(8,128)(2,1)}), bf16[8,384,256]{2,1,0:T(8,128)(2,1)S(1)}, u32[]{:S(2)}, u32[]{:S(2)}) %all-to-all-start.4) | async-done | bytes 1572896 | tf_op jit(solution)/shard_map/all_to_all | solution.py:18
  183.0 0.7 add_convert_fusion
  183.7 3.4 %all-to-all-start.5 = ((bf16[1,16,24,256]{3,2,0,1:T(8,128)(2,1)}), bf16[1,16,24,256]{3,2,0,1:T(8,128)(2,1)S(1)}, u32[]{:S(2)}, u32[]{:S(2)}) async-start(bf16[1,16,24,256]{3,2,0,1:T(8,128)(2,1)} %add_convert_fusion), calls=%async_computation.5 | async-start | bytes 393216 | tf_op jit(solution)/shard_map/all_to_all | solution.py:118
  187.2 6.3 %all-to-all-done.5 = bf16[1,16,24,256]{3,2,0,1:T(8,128)(2,1)S(1)} async-done(((bf16[1,16,24,256]{3,2,0,1:T(8,128)(2,1)}), bf16[1,16,24,256]{3,2,0,1:T(8,128)(2,1)S(1)}, u32[]{:S(2)}, u32[]{:S(2)}) %all-to-all-start.5) | async-done | bytes 196640 | tf_op jit(solution)/shard_map/all_to_all | solution.py:118
  194.1 12.9 %all_to_all.46 = bf16[1,16,24,256]{3,2,0,1:T(8,128)(2,1)S(1)} all-to-all(bf16[1,16,24,256]{3,2,0,1:T(8,128)(2,1)S(1)} %fusion.74), channel_id=1, replica_groups=mesh['client'=16,'tensor'=8,'sdata'=2] {'client'}, dimensions={1} | all-to-all | bytes 393216 | tf_op jit(solution)/shard_map/all_to_all | solution.py:114
  207.3 1.3 stack.19
  208.6 6.9 %all-to-all-start.7 = ((bf16[8,1,384,256]{2,3,1,0:T(8,128)(2,1)}), bf16[8,1,384,256]{2,3,1,0:T(8,128)(2,1)S(1)}, u32[]{:S(2)}, u32[]{:S(2)}) async-start(bf16[8,1,384,256]{2,3,1,0:T(8,128)(2,1)} %stack.19), calls=%async_computation.7 | async-start | bytes 3145728 | tf_op jit(solution)/shard_map/all_to_all | solution.py:141
  215.5 18.4 %all-to-all-done.7 = bf16[8,1,384,256]{2,3,1,0:T(8,128)(2,1)S(1)} async-done(((bf16[8,1,384,256]{2,3,1,0:T(8,128)(2,1)}), bf16[8,1,384,256]{2,3,1,0:T(8,128)(2,1)S(1)}, u32[]{:S(2)}, u32[]{:S(2)}) %all-to-all-start.7) | async-done | bytes 1572896 | tf_op jit(solution)/shard_map/all_to_all | solution.py:141
  233.9 0.8 convolution_convert_fusion.7
  234.7 0.7 convolution_convert_fusion.1
  235.4 4.1 %convolution_convert_fusion.3 = bf16[2048,64]{0,1:T(8,128)(2,1)} fusion(bf16[64,4,384]{2,0,1:T(8,128)(2,1)S(1)} %bitcast.264, f32[4,384]{1,0:T(4,128)S(1)} %fusion.93, f32[4,384]{1,0:T(4,128)S(1)} %get-tuple-element.29, f32[384,384,4]{1,0,2:T(8,128)} %copy-done.3, pred[384,384]{0,1:T(8,128)(4,1)S(1)} %iota_compare_fusion, bf16[384,2048]{1,0:T(8,128)(2,1)} %param.12, ...), kind=kOutput, calls=%fused_computation.33 | convolution fusion | flops 182411264 | bytes 4560384 | tf_op jit(solution)/shard_map/transpose(jvp())/dot_general | solution.py:64
  239.5 2.7 fusion.11
  242.3 1.8 fusion.51
  244.1 2.0 broadcast_multiply_fusion
  246.1 1.2 copy.65
  247.3 1.8 fusion.101
  249.2 0.9 multiply_bitcast_fusion
  250.1 2.2 convolution_convert_fusion.4
  252.4 1.2 copy.64
  253.6 1.2 pad_add_fusion
  254.9 2.3 convolution_convert_fusion.2
  257.2 1.2 pad_maximum_fusion
  258.4 66.2 %all_to_all.47 = bf16[32,64,640]{2,1,0:T(8,128)(2,1)S(1)} all-to-all(bf16[32,64,640]{2,1,0:T(8,128)(2,1)S(1)} %pad_maximum_fusion), channel_id=1, replica_groups=mesh['client'=16,'tensor'=8,'sdata'=2] {'client','sdata'}, dimensions={0} | all-to-all | bytes 5242880 | tf_op jit(solution)/shard_map/all_to_all | solution.py:18
  325.0 0.7 fusion.104
  325.7 0.6 fusion.103
  (105 shorter events, 4.6 us)
Async XLA Ops:
  0.6 144.3 %copy-start = (bf16[1,2048,512]{2,1,0:T(8,128)(2,1)S(1)}, bf16[1,2048,512]{2,1,0:T(8,128)(2,1)}, u32[]{:S(2)}) copy-start(bf16[1,2048,512]{2,1,0:T(8,128)(2,1)} %param.20) | copy-start | bytes 6291460
  0.7 5.4 %copy-start.5 = (bf16[384,2048]{1,0:T(8,128)(2,1)S(1)}, bf16[384,2048]{1,0:T(8,128)(2,1)}, u32[]{:S(2)}) copy-start(bf16[384,2048]{1,0:T(8,128)(2,1)} %param.12) | copy-start | bytes 4718596
  0.7 5.4 %copy-start.32 = (bf16[1,2048,64]{1,2,0:T(8,128)(2,1)S(1)}, bf16[1,2048,64]{1,2,0:T(8,128)(2,1)}, u32[]{:S(2)}) copy-start(bf16[1,2048,64]{1,2,0:T(8,128)(2,1)} %param.15) | copy-start | bytes 786436
  2.7 6.9 %copy-start.27 = (f32[384]{0:T(512)}, f32[384]{0:T(512)S(1)}, u32[]{:S(2)}) copy-start(f32[384]{0:T(512)S(1)} %add_rsqrt_fusion.1) | copy-start | bytes 4612
  3.4 6.1 %copy-start.24 = (f32[1,2048]{1,0:T(1,128)}, f32[1,2048]{1,0:T(1,128)S(1)}, u32[]{:S(2)}) copy-start(f32[1,2048]{1,0:T(1,128)S(1)} %mul.299) | copy-start | bytes 24580
  6.2 2.0 copy-start.9
  6.8 0.6 copy-start.16
  9.6 2.9 copy-start.17
  9.6 2.9 copy-start.19
  9.6 2.9 copy-start.20
  12.4 1.4 copy-start.18
  12.5 1.4 copy-start.21
  12.6 0.7 copy-start.12
  13.2 1.1 copy-start.34
  13.8 1.4 copy-start.3
  14.4 1.5 copy-start.10
  15.2 2.5 copy-start.14
  17.8 24.9 %all-to-all-start = ((bf16[8,384,256]{2,1,0:T(8,128)(2,1)}), bf16[8,384,256]{2,1,0:T(8,128)(2,1)}, u32[]{:S(2)}, u32[]{:S(2)}) async-start(bf16[8,384,256]{2,1,0:T(8,128)(2,1)} %bitcast.234), calls=%async_computation | async-start | bytes 3145728 | tf_op jit(solution)/shard_map/all_to_all | solution.py:18
  24.2 30.0 %copy-start.33 = (s32[16]{0:T(128)S(1)}, s32[16]{0:T(128)}, u32[]{:S(2)}) copy-start(s32[16]{0:T(128)} %param.23) | copy-start | bytes 196
  46.1 20.7 %all-to-all-start.1 = ((bf16[2,16,24,256]{3,2,0,1:T(8,128)(2,1)}), bf16[2,16,24,256]{3,2,0,1:T(8,128)(2,1)S(1)}, u32[]{:S(2)}, u32[]{:S(2)}) async-start(bf16[2,16,24,256]{3,2,0,1:T(8,128)(2,1)} %pad_maximum_fusion.1), calls=%async_computation.1 | async-start | bytes 786432 | tf_op jit(solution)/shard_map/all_to_all | solution.py:114
  80.9 7.3 %copy-start.23 = (bf16[1,2048]{1,0:T(2,128)(2,1)S(1)}, bf16[1,2048]{1,0:T(2,128)(2,1)}, u32[]{:S(2)}) copy-start(bf16[1,2048]{1,0:T(2,128)(2,1)} %param.18) | copy-start | bytes 12292
  80.9 42.6 %all-to-all-start.3 = ((bf16[8,2,384,256]{3,2,1,0:T(8,128)(2,1)}), bf16[8,2,384,256]{3,2,1,0:T(8,128)(2,1)}, u32[]{:S(2)}, u32[]{:S(2)}) async-start(bf16[8,2,384,256]{3,2,1,0:T(8,128)(2,1)} %stack.18), calls=%async_computation.3 | async-start | bytes 6291456 | tf_op jit(solution)/shard_map/all_to_all | solution.py:141
  138.0 2.1 copy-start.31
  140.0 2.0 copy-start.7
  140.1 2.0 copy-start.8
  140.1 2.8 copy-start.30
  151.2 4.6 %copy-start.2 = (f32[384,2048]{1,0:T(8,128)S(1)}, f32[384,2048]{1,0:T(8,128)}, u32[]{:S(2)}) copy-start(f32[384,2048]{1,0:T(8,128)} %copy.63) | copy-start | bytes 9437188
  157.7 25.1 %all-to-all-start.4 = ((bf16[8,384,256]{2,1,0:T(8,128)(2,1)}), bf16[8,384,256]{2,1,0:T(8,128)(2,1)S(1)}, u32[]{:S(2)}, u32[]{:S(2)}) async-start(bf16[8,384,256]{2,1,0:T(8,128)(2,1)} %bitcast.227), calls=%async_computation.4 | async-start | bytes 3145728 | tf_op jit(solution)/shard_map/all_to_all | solution.py:18
  183.7 9.8 %all-to-all-start.5 = ((bf16[1,16,24,256]{3,2,0,1:T(8,128)(2,1)}), bf16[1,16,24,256]{3,2,0,1:T(8,128)(2,1)S(1)}, u32[]{:S(2)}, u32[]{:S(2)}) async-start(bf16[1,16,24,256]{3,2,0,1:T(8,128)(2,1)} %add_convert_fusion), calls=%async_computation.5 | async-start | bytes 393216 | tf_op jit(solution)/shard_map/all_to_all | solution.py:118
  207.2 26.6 %copy-start.11 = (bf16[1,2048,256]{2,1,0:T(8,128)(2,1)S(1)}, bf16[1,2048,256]{2,1,0:T(8,128)(2,1)}, u32[]{:S(2)}) copy-start(bf16[1,2048,256]{2,1,0:T(8,128)(2,1)} %param.17) | copy-start | bytes 3145732
  208.6 25.3 %all-to-all-start.7 = ((bf16[8,1,384,256]{2,3,1,0:T(8,128)(2,1)}), bf16[8,1,384,256]{2,3,1,0:T(8,128)(2,1)S(1)}, u32[]{:S(2)}, u32[]{:S(2)}) async-start(bf16[8,1,384,256]{2,3,1,0:T(8,128)(2,1)} %stack.19), calls=%async_computation.7 | async-start | bytes 3145728 | tf_op jit(solution)/shard_map/all_to_all | solution.py:141
  215.5 19.2 %copy-start.15 = (bf16[64,4,384]{2,0,1:T(8,128)(2,1)S(1)}, bf16[64,4,384]{2,0,1:T(8,128)(2,1)}, u32[]{:S(2)}) copy-start(bf16[64,4,384]{2,0,1:T(8,128)(2,1)} %copy-done.14) | copy-start | bytes 589828
  234.6 0.8 copy-start.25
  234.7 0.8 copy-start.28
  235.4 4.1 %copy-start.35 = (bf16[384,64,1]{0,1,2:T(8,128)(2,1)S(1)}, bf16[384,64,1]{0,1,2:T(8,128)(2,1)}, u32[]{:S(2)}) copy-start(bf16[384,64,1]{0,1,2:T(8,128)(2,1)} %fusion.57) | copy-start | bytes 147460
  239.5 2.7 copy-start.4
  239.5 2.7 copy-start.13
  242.2 1.9 copy-start.22
  244.1 6.0 %copy-start.6 = (bf16[384,2048]{1,0:T(8,128)(2,1)S(1)}, bf16[384,2048]{1,0:T(8,128)(2,1)}, u32[]{:S(2)}) copy-start(bf16[384,2048]{1,0:T(8,128)(2,1)} %param.12) | copy-start | bytes 4718596
  250.1 4.8 %copy-start.26 = (f32[1,2048]{1,0:T(1,128)S(1)}, f32[1,2048]{1,0:T(1,128)}, u32[]{:S(2)}) copy-start(f32[1,2048]{1,0:T(1,128)} %copy-done.24) | copy-start | bytes 24580
  250.1 4.8 %copy-start.29 = (f32[384]{0:T(512)S(1)}, f32[384]{0:T(512)}, u32[]{:S(2)}) copy-start(f32[384]{0:T(512)} %copy-done.27) | copy-start | bytes 4612
  258.4 67.9 %copy-start.1 = (bf16[1,2048,512]{2,1,0:T(8,128)(2,1)S(1)}, bf16[1,2048,512]{2,1,0:T(8,128)(2,1)}, u32[]{:S(2)}) copy-start(bf16[1,2048,512]{2,1,0:T(8,128)(2,1)} %param.20) | copy-start | bytes 6291460
